TPU v7x, 32 devices: a whole 2x2x4 slice. The times are simulated.
32 devices in a mesh: face: 16 (over z, y, core), sub: 2 (over x).
Axes of the slice: x: 2, y: 2, z: 4, core: 2. Of those that a mesh axis runs over, the one named last changes fastest.
Arguments:
- prognostic: bfloat16 [3, 2048, 16, 128], P(None, ('face', 'sub')), may hold values from -4 to 4
- metric: float32 [4, 2048, 16], P(None, ('face', 'sub')), may hold values from -0.35 to 1.6, as said below
- coriolis: float32 [2048, 16], P(('face', 'sub')), may hold values from -1.5 to 1.5
- node_point: int32 [2048, 16], P(('face', 'sub')), may hold values from 0 to 678, as said below
- send_point: int32 [6784], P(('face', 'sub')), may hold values from 0 to 678, as said below
- recv_point: int32 [6784], P(('face', 'sub')), may hold values from 0 to 678, as said below
Outputs:
- advanced: bfloat16 [3, 2048, 16, 128], P(None, ('face', 'sub'))
Inputs may be any that keep to these rules, and one draw needn't show every extreme that they name: `node_point`: each device's numbers are its 679 local points; element nodes that are the same point of the surface on one device carry the same number. `send_point`: on every device the 212 slots form groups in this order: 7 slots of offset +1, 7 of offset -1, 97 of offset +8, 97 of offset -8, then one slot each of offsets 8 + 1, -8 - 1, 7, 1 - 8. A slot names the sender's point that the device at curve index d + o, taken modulo 32, shares. Every slot is used. `recv_point`: slot s of device d names the local point that is the same surface point as the sender's slot s, the sender being the device at d minus the slot's group offset modulo 32. The copies of every shared point are linked between every two devices that hold them. `metric`: entries 0 and 3 lie in [0.6, 1.6], entries 1 and 2 in [-0.35, 0.35].
All inputs are finite; a program needn't handle non-finite values.
Results may differ from a plain program's by a relative error of at most 0.007.
Values sent between devices are 32-bit elements; how exact they have to be, the bound alone decides.
A program may use at most 64 MiB of HBM per device.

v0:
```python
import math

import jax
import jax.numpy as jnp
import numpy as np
from jax import lax
from jax.sharding import PartitionSpec as P

BX = 32
BY = 2
PTS = 679


STEP_SIZE = 0.1


def from_behind(value, axis, steps):
    count = lax.axis_size(axis)
    pairs = [(source, (source + steps) % count) for source in range(count)]
    return lax.ppermute(value, axis, pairs)


def gll_tables():
    abscissa = np.array([-1.0, -math.sqrt(0.2), math.sqrt(0.2), 1.0])
    legendre = 0.5 * (5.0 * abscissa * abscissa * abscissa - 3.0 * abscissa)
    derivative = np.zeros((4, 4))
    for target in range(4):
        for source in range(4):
            if target != source:
                derivative[target, source] = legendre[target] / (
                    legendre[source] * (abscissa[target] - abscissa[source])
                )
    derivative[0, 0] = -3.0
    derivative[3, 3] = 3.0
    weights = np.array([1.0, 5.0, 5.0, 1.0]) / 6.0
    return (derivative, weights)


def along_cols(values, derivative):
    return jnp.einsum("aj,erjl->eral", derivative, values, precision=lax.Precision.HIGHEST)


def along_rows(values, derivative):
    return jnp.einsum("aj,ejcl->eacl", derivative, values, precision=lax.Precision.HIGHEST)


def element_tendency(fields, metric, coriolis):
    elements = fields.shape[1]
    levels = fields.shape[3]
    deriv_table, weight_table = gll_tables()
    derivative = jnp.asarray(deriv_table, dtype=jnp.float32)
    weights = jnp.asarray(weight_table, dtype=jnp.float32)
    shaped = fields.reshape(3, elements, 4, 4, levels)
    veloc_one = shaped[0]
    veloc_two = shaped[1]
    geopot = shaped[2]
    inverse = metric.reshape(4, elements, 4, 4, 1)
    inv_aa = inverse[0]
    inv_ab = inverse[1]
    inv_ba = inverse[2]
    inv_bb = inverse[3]
    jacobian_inv = inv_aa * inv_bb - inv_ab * inv_ba
    energy = 0.5 * (veloc_one * veloc_one + veloc_two * veloc_two) + geopot
    ref_one = along_cols(energy, derivative)
    ref_two = along_rows(energy, derivative)
    grad_one = inv_aa * ref_one + inv_ba * ref_two
    grad_two = inv_ab * ref_one + inv_bb * ref_two
    cov_one = (inv_bb * veloc_one - inv_ba * veloc_two) / jacobian_inv
    cov_two = (inv_aa * veloc_two - inv_ab * veloc_one) / jacobian_inv
    vorticity = jacobian_inv * (along_cols(cov_two, derivative) - along_rows(cov_one, derivative))
    absolute = vorticity + coriolis.reshape(elements, 4, 4, 1)
    flux_one = geopot * veloc_one
    flux_two = geopot * veloc_two
    contra_one = (inv_aa * flux_one + inv_ab * flux_two) / jacobian_inv
    contra_two = (inv_ba * flux_one + inv_bb * flux_two) / jacobian_inv
    divergence = jacobian_inv * (
        along_cols(contra_one, derivative) + along_rows(contra_two, derivative)
    )
    tendency = jnp.stack(
        [absolute * veloc_two - grad_one, -absolute * veloc_one - grad_two, -divergence]
    )
    mass_weight = (weights[:, None] * weights[None, :])[None] / jacobian_inv[..., 0]
    return (tendency.reshape(3, elements, 16, levels), mass_weight.reshape(elements, 16))


def link_groups(lap_blocks):
    side_points = 3 * BY + 1
    top_points = 3 * BX + 1
    group_sizes = [
        (1, side_points),
        (-1, side_points),
        (lap_blocks, top_points),
        (-lap_blocks, top_points),
        (lap_blocks + 1, 1),
        (-lap_blocks - 1, 1),
        (lap_blocks - 1, 1),
        (1 - lap_blocks, 1),
    ]
    groups = []
    first_slot = 0
    for offset, slot_count in group_sizes:
        groups.append((offset, first_slot, slot_count))
        first_slot = first_slot + slot_count
    return groups


def select_table(indices, count):
    return (indices[:, None] == jnp.arange(count, dtype=jnp.int32)[None, :]).astype(jnp.bfloat16)


def split_dot(form, table, values):
    upper = values.astype(jnp.bfloat16)
    lower = (values - upper.astype(jnp.float32)).astype(jnp.bfloat16)
    first = jnp.einsum(form, table, upper, preferred_element_type=jnp.float32)
    return first + jnp.einsum(form, table, lower, preferred_element_type=jnp.float32)


def local(prognostic, metric, coriolis, node_point, send_point, recv_point):
    elements = prognostic.shape[1]
    levels = prognostic.shape[3]
    fields = prognostic.astype(jnp.float32)
    tendency, mass_weight = element_tendency(fields, metric, coriolis)
    point_ids = node_point.reshape(-1)
    weighted = (tendency * mass_weight[None, :, :, None]).reshape(3, elements * 16, levels)
    node_table = select_table(point_ids, PTS)
    partial_value = split_dot("np,fnl->fpl", node_table, weighted)
    weight = split_dot("np,n->p", node_table, mass_weight.reshape(-1))
    send_table = select_table(send_point, PTS)
    outgoing = split_dot("sp,fpl->fsl", send_table, partial_value)
    out_weight = split_dot("sp,p->s", send_table, weight)
    groups = link_groups(4 * lax.axis_size("sub"))

    def group_slice(values, masses, group_index):
        offset, first_slot, slot_count = groups[group_index]
        return (
            values[:, first_slot : first_slot + slot_count, :],
            masses[first_slot : first_slot + slot_count],
        )

    def split_bundle(bundle, members):
        result = {}
        cursor = 0
        for group_index in members:
            slot_count = groups[group_index][2]
            result[group_index] = (
                bundle[0][:, cursor : cursor + slot_count, :],
                bundle[1][cursor : cursor + slot_count],
            )
            cursor = cursor + slot_count
        return result

    arrived = [None] * 8
    lap_blocks = groups[2][0]
    landed_vertical = {}
    for direction, members in ((1, (2, 4, 6)), (-1, (3, 5, 7))):
        sections = [group_slice(outgoing, out_weight, group_index) for group_index in members]
        values_cat = jnp.concatenate([section[0] for section in sections], axis=1)
        masses_cat = jnp.concatenate([section[1] for section in sections], axis=0)
        landed = from_behind((values_cat, masses_cat), ("face", "sub"), direction * lap_blocks)
        landed_vertical[direction] = split_bundle(landed, members)
    from_below = landed_vertical[1]
    from_above = landed_vertical[-1]
    arrived[2] = from_below[2]
    arrived[3] = from_above[3]
    plans = (
        (1, (0, 4, 7), (group_slice(outgoing, out_weight, 0), from_below[4], from_above[7])),
        (-1, (1, 6, 5), (group_slice(outgoing, out_weight, 1), from_below[6], from_above[5])),
    )
    for direction, members, sections in plans:
        values_cat = jnp.concatenate([section[0] for section in sections], axis=1)
        masses_cat = jnp.concatenate([section[1] for section in sections], axis=0)
        landed = from_behind((values_cat, masses_cat), ("face", "sub"), direction)
        pieces_back = split_bundle(landed, members)
        for group_index in members:
            arrived[group_index] = pieces_back[group_index]
    received = jnp.concatenate([arrived[group_index][0] for group_index in range(8)], axis=1)
    received_weight = jnp.concatenate([arrived[group_index][1] for group_index in range(8)], axis=0)
    recv_table = select_table(recv_point, PTS)
    total = partial_value + split_dot("sp,fsl->fpl", recv_table, received)
    total_weight = weight + split_dot("sp,s->p", recv_table, received_weight)
    point_average = total / total_weight[None, :, None]
    averaged = split_dot("np,fpl->fnl", node_table, point_average)
    advanced = fields + STEP_SIZE * averaged.reshape(3, elements, 16, levels)
    return advanced.astype(jnp.bfloat16)


def solution(mesh):
    placed = (
        P(None, ("face", "sub"), None, None),
        P(None, ("face", "sub"), None),
        P(("face", "sub"), None),
        P(("face", "sub"), None),
        P(("face", "sub")),
        P(("face", "sub")),
    )
    return jax.shard_map(
        local,
        mesh=mesh,
        in_specs=placed,
        out_specs=P(None, ("face", "sub"), None, None),
        check_vma=False,
    )
```

profile of v0, /device:TPU:0, one launch (start us, length us, event | category | flops | bytes accessed | tf_op | source)
XLA Modules:
  0.0 79.5 jit_solution(14302513953383177414)
XLA Ops:
  0.0 0.8 copy.62
  0.9 1.2 %fusion.88 = (f32[1,64,16,128]{3,2,1,0:T(8,128)S(1)}, f32[1,64,16,128]{3,2,1,0:T(8,128)S(1)}, f32[1,64,16,128]{3,2,1,0:T(8,128)S(1)}) fusion(bf16[3,64,16,128]{3,2,1,0:T(8,128)(2,1)} %param.8), kind=kLoop, calls=%fused_computation.112 | loop fusion | bytes 3145728 | tf_op jit(solution)/shard_map/slice | solution.py:54
  2.4 0.8 copy.49
  4.1 1.0 %multiply_add_fusion = (f32[64,4,4,128]{3,2,1,0:T(4,128)S(1)}, f32[64,4,4,128]{3,2,1,0:T(4,128)S(1)}, f32[64,4,4,128]{3,2,1,0:T(4,128)S(1)}) fusion(f32[64,4,4,128]{3,2,1,0:T(4,128)S(1)} %bitcast.119, f32[64,4,4,128]{3,2,1,0:T(4,128)S(1)} %bitcast.115, f32[64,4,4,128]{3,2,1,0:T(4,128)S(1)} %bitcast.111, f32[64,4,4]{2,1,0:T(4,128)S(1)} %copy.47, ...), kind=kLoop, calls=%fused_computation.66 | loop fusion | flops 1966080 | bytes 3158016 | tf_op jit(solution)/shard_map/add | solution.py:63
  5.1 1.8 %fusion.52 = f32[64,4,128,4]{2,3,1,0:T(4,128)} fusion(f32[4,4,1,1]{1,0,3,2:T(4,128)S(1)} %copy-done.5, f32[64,4,4,128]{3,2,1,0:T(4,128)S(1)} %get-tuple-element.13), kind=kOutput, calls=%fused_computation.56 | convolution fusion | flops 6291456 | bytes 1048640 | tf_op jit(solution)/shard_map/aj,ejcl->eacl/dot_general | solution.py:44
  7.0 1.0 %fusion.56 = f32[64,4,128,4]{2,3,1,0:T(4,128)S(1)} fusion(f32[4,4,1,1]{1,0,3,2:T(4,128)S(1)} %copy-done.5, f32[64,4,4,128]{3,2,1,0:T(4,128)S(1)} %get-tuple-element.14), kind=kOutput, calls=%fused_computation.60 | convolution fusion | flops 6291456 | bytes 1048640 | tf_op jit(solution)/shard_map/aj,ejcl->eacl/dot_general | solution.py:44
  8.8 1.0 %fusion.54 = f32[64,4,128,4]{2,3,1,0:T(4,128)S(1)} fusion(f32[4,4,1,1]{1,0,3,2:T(4,128)S(1)} %copy-done.5, f32[64,4,4,128]{3,2,1,0:T(4,128)S(1)} %get-tuple-element.12), kind=kOutput, calls=%fused_computation.58 | convolution fusion | flops 6291456 | bytes 1048640 | tf_op jit(solution)/shard_map/aj,ejcl->eacl/dot_general | solution.py:44
  9.8 0.8 %broadcast_multiply_fusion = f32[4,4]{1,0:T(4,128)S(1)} fusion(f32[4]{0:T(128)} %constant.9.clone), kind=kLoop, calls=%fused_computation.104 | loop fusion | flops 16 | bytes 80 | tf_op jit(solution)/shard_map/mul | solution.py:82
  11.3 1.6 %div.61 = f32[1024]{0:T(1024)} reshape(f32[64,4,4]{2,1,0:T(4,128)} %div.60) | data formatting | bytes 8192 | tf_op jit(solution)/shard_map/div | solution.py:82
  13.6 0.8 %sub.62 = f32[1024]{0:T(1024)S(1)} reshape(f32[1,64,16]{2,1,0:T(8,128)} %copy.61) | data formatting | bytes 8192 | tf_op jit(solution)/shard_map/sub | solution.py:62
  18.4 1.4 %div.58 = f32[1024]{0:T(1024)} reshape(f32[64,16]{1,0:T(8,128)} %div.57) | data formatting | bytes 8192 | tf_op jit(solution)/shard_map/div | solution.py:82
  19.8 3.8 %fusion.30 = f32[64,4,4,128]{3,2,1,0:T(4,128)S(1)} fusion(f32[4,4,1,1]{1,0,3,2:T(4,128)S(1)} %copy-done.5, f32[64,4,128,4]{2,3,1,0:T(4,128)} %fusion.52, f32[64,4,4]{2,1,0:T(4,128)} %copy.49, f32[64,4,4]{2,1,0:T(4,128)} %copy.48, f32[64,4,4]{2,1,0:T(4,128)S(1)} %copy.47, f32[64,4,4,128]{3,2,1,0:T(4,128)S(1)} %bitcast.120, ...), kind=kOutput, calls=%fused_computation.27 | convolution fusion | flops 7471104 | bytes 2633792 | tf_op jit(solution)/shard_map/aj,erjl->eral/dot_general | solution.py:40
  23.7 2.5 %fusion.33 = f32[64,4,4,128]{3,2,1,0:T(4,128)S(1)} fusion(f32[4,4,1,1]{1,0,3,2:T(4,128)S(1)} %copy-done.5, f32[64,4,128,4]{2,3,1,0:T(4,128)S(1)} %fusion.56, f32[64,4,4,128]{3,2,1,0:T(4,128)S(1)} %bitcast.113, f32[64,4,4,128]{3,2,1,0:T(4,128)S(1)} %bitcast.117, f32[64,4,4]{2,1,0:T(4,128)S(1)} %copy-done.3, f32[64,4,4]{2,1,0:T(4,128)S(1)} %copy-done.1, ...), kind=kOutput, calls=%fused_computation.31 | convolution fusion | flops 7208960 | bytes 2113600 | tf_op jit(solution)/shard_map/aj,erjl->eral/dot_general | solution.py:40
  26.2 2.1 %fusion.51 = (f32[64,4,4,128]{3,2,1,0:T(4,128)S(1)}, f32[64,4,4,128]{3,2,1,0:T(4,128)S(1)}) fusion(f32[64,4,4,128]{3,2,1,0:T(4,128)S(1)} %fusion.33, f32[64,4,4,128]{3,2,1,0:T(4,128)S(1)} %bitcast.118, f32[64,4,128,4]{2,3,1,0:T(4,128)S(1)} %fusion.54, f32[64,4,4]{2,1,0:T(4,128)S(1)} %copy-done.2, f32[64,4,4]{2,1,0:T(4,128)S(1)} %copy.51, ...), kind=kOutput, calls=%fused_computation.55 | convolution fusion | flops 7733248 | bytes 3686464 | tf_op jit(solution)/shard_map/aj,erjl->eral/dot_general | solution.py:40
  28.3 1.0 %fusion.7 = f32[3,128,679]{1,2,0:T(8,128)S(1)} fusion(s32[1024]{0:T(1024)S(1)} %eq.20, f32[1,1024,128]{2,1,0:T(8,128)S(1)} %bitcast.139, f32[1,1024,128]{2,1,0:T(8,128)S(1)} %bitcast.143, f32[1,1024,128]{2,1,0:T(8,128)S(1)} %bitcast.141, f32[1024]{0:T(1024)S(1)} %get-tuple-element.41), kind=kOutput, calls=%fused_computation.6 | convolution fusion | flops 537435136 | bytes 2624000 | tf_op jit(solution)/shard_map/np,fnl->fpl/dot_general | solution.py:115
  29.3 1.0 %fusion.22 = f32[3,679,128]{2,1,0:T(8,128)S(1)} fusion(f32[3,128,679]{1,2,0:T(8,128)S(1)} %fusion.7, s32[1024]{0:T(1024)S(1)} %eq.20, f32[1,1024,128]{2,1,0:T(8,128)S(1)} %bitcast.140, f32[1,1024,128]{2,1,0:T(8,128)S(1)} %bitcast.144, f32[1,1024,128]{2,1,0:T(8,128)S(1)} %bitcast.142, f32[1024]{0:T(1024)S(1)} %get-tuple-element.41), kind=kOutput, calls=%fused_computation.19 | convolution fusion | flops 536516224 | bytes 3666944 | tf_op jit(solution)/shard_map/np,fnl->fpl/dot_general | solution.py:114
  31.1 5.1 %collective-permute-start.1 = (f32[3,99,128]{2,1,0:T(8,128)S(1)}, f32[3,99,128]{2,1,0:T(8,128)S(1)}, u32[]{:S(2)}, u32[]{:S(2)}) collective-permute-start(f32[3,99,128]{2,1,0:T(8,128)S(1)} %pad_maximum_fusion.1), channel_id=1, source_target_pairs={{0,24},{1,25},{2,26},{3,27},{4,28},{5,29},{6,30},{7,31},{8,0},{9,1... | collective-permute-start | bytes 456200 | tf_op jit(solution)/shard_map/ppermute | solution.py:20
  38.9 1.4 %pad_maximum_fusion.5 = f32[99]{0:T(128)S(1)} fusion(f32[1]{0:T(128)} %get-tuple-element.47, f32[1]{0:T(128)} %get-tuple-element.48, f32[97]{0:T(128)S(1)} %get-tuple-element.45), kind=kLoop, calls=%fused_computation.106 | loop fusion | flops 198 | bytes 792 | tf_op jit(solution)/shard_map/concatenate | solution.py:158
  40.3 3.8 %collective-permute-start.5 = (f32[99]{0:T(128)S(1)}, f32[99]{0:T(128)S(1)}, u32[]{:S(2)}, u32[]{:S(2)}) collective-permute-start(f32[99]{0:T(128)S(1)} %pad_maximum_fusion.5), channel_id=1, source_target_pairs={{0,24},{1,25},{2,26},{3,27},{4,28},{5,29},{6,30},{7,31},{8,0},{9,1... | collective-permute-start | bytes 1196 | tf_op jit(solution)/shard_map/ppermute | solution.py:20
  44.1 1.3 %pad_maximum_fusion.4 = f32[99]{0:T(128)S(1)} fusion(f32[1]{0:T(128)} %get-tuple-element.49, f32[1]{0:T(128)} %get-tuple-element.46, f32[97]{0:T(128)S(1)} %get-tuple-element.44), kind=kLoop, calls=%fused_computation.105 | loop fusion | flops 198 | bytes 792 | tf_op jit(solution)/shard_map/concatenate | solution.py:158
  46.2 4.6 %collective-permute-done.4 = f32[99]{0:T(128)S(1)} collective-permute-done((f32[99]{0:T(128)S(1)}, f32[99]{0:T(128)S(1)}, u32[]{:S(2)}, u32[]{:S(2)}) %collective-permute-start.4) | collective-permute-done | bytes 428 | tf_op jit(solution)/shard_map/ppermute | solution.py:20
  51.4 1.4 %pad_maximum_fusion.6 = f32[9]{0:T(128)S(1)} fusion(f32[1]{0:T(128)} %get-tuple-element.57, f32[1]{0:T(128)} %get-tuple-element.55, f32[7]{0:T(128)S(1)} %get-tuple-element.43), kind=kLoop, calls=%fused_computation.107 | loop fusion | flops 18 | bytes 72 | tf_op jit(solution)/shard_map/concatenate | solution.py:171
  52.8 1.5 %collective-permute-start.6 = (f32[9]{0:T(128)S(1)}, f32[9]{0:T(128)S(1)}, u32[]{:S(2)}, u32[]{:S(2)}) collective-permute-start(f32[9]{0:T(128)S(1)} %pad_maximum_fusion.6), channel_id=1, source_target_pairs={{0,1},{1,2},{2,3},{3,4},{4,5},{5,6},{6,7},{7,8},{8,9},{9,10},{10,1... | collective-permute-start | bytes 116 | tf_op jit(solution)/shard_map/ppermute | solution.py:20
  54.3 1.4 %pad_maximum_fusion.7 = f32[9]{0:T(128)S(1)} fusion(f32[1]{0:T(128)} %get-tuple-element.56, f32[1]{0:T(128)} %get-tuple-element.54, f32[7]{0:T(128)S(1)} %get-tuple-element.42), kind=kLoop, calls=%fused_computation.108 | loop fusion | flops 18 | bytes 72 | tf_op jit(solution)/shard_map/concatenate | solution.py:171
  55.7 3.8 %collective-permute-start.7 = (f32[9]{0:T(128)S(1)}, f32[9]{0:T(128)S(1)}, u32[]{:S(2)}, u32[]{:S(2)}) collective-permute-start(f32[9]{0:T(128)S(1)} %pad_maximum_fusion.7), channel_id=1, source_target_pairs={{0,31},{1,0},{2,1},{3,2},{4,3},{5,4},{6,5},{7,6},{8,7},{9,8},{10,9... | collective-permute-start | bytes 116 | tf_op jit(solution)/shard_map/ppermute | solution.py:20
  61.4 2.7 %concatenate.41 = f32[212]{0:T(256)S(1)} concatenate(f32[7]{0:T(128)S(1)} %bitcast.135, f32[7]{0:T(128)S(1)} %bitcast.136, f32[97]{0:T(128)S(1)} %bitcast.134, f32[97]{0:T(128)S(1)} %bitcast.133, f32[1]{0:T(128)} %get-tuple-element.51, f32[1]{0:T(128)} %get-tuple-element.53, f32[1]{0:T(128)} %get-tuple-element.52, f32[1]{0:T(128)} %get-tuple-element.50), dimensions={0} | concatenate | bytes 1696 | tf_op jit(solution)/shard_map/concatenate | solution.py:177
  64.9 5.6 %collective-permute-start.3 = (f32[3,9,128]{2,1,0:T(8,128)S(1)}, f32[3,9,128]{2,1,0:T(8,128)S(1)}, u32[]{:S(2)}, u32[]{:S(2)}) collective-permute-start(f32[3,9,128]{2,1,0:T(8,128)S(1)} %pad_maximum_fusion.3), channel_id=1, source_target_pairs={{0,31},{1,0},{2,1},{3,2},{4,3},{5,4},{6,5},{7,6},{8,7},{9,8},{10,9... | collective-permute-start | bytes 41480 | tf_op jit(solution)/shard_map/ppermute | solution.py:20
  70.4 1.3 %collective-permute-done.2 = f32[3,9,128]{2,1,0:T(8,128)S(1)} collective-permute-done((f32[3,9,128]{2,1,0:T(8,128)S(1)}, f32[3,9,128]{2,1,0:T(8,128)S(1)}, u32[]{:S(2)}, u32[]{:S(2)}) %collective-permute-start.2) | collective-permute-done | bytes 13856 | tf_op jit(solution)/shard_map/ppermute | solution.py:20
  73.5 0.9 %fusion.3 = f32[3,128,1024]{2,1,0:T(8,128)S(1)} fusion(s32[1024]{0:T(1024)S(1)} %eq.20, f32[3,679,128]{2,1,0:T(8,128)S(1)} %fusion.27), kind=kOutput, calls=%fused_computation.4 | convolution fusion | flops 535725568 | bytes 2619904 | tf_op jit(solution)/shard_map/np,fpl->fnl/dot_general | solution.py:115
  74.4 2.1 %multiply_bitcast_fusion = f32[3,1024,128]{1,2,0:T(8,128)} fusion(f32[3,128,1024]{2,1,0:T(8,128)S(1)} %fusion.3, s32[1024]{0:T(1024)S(1)} %eq.20, f32[3,679,128]{2,1,0:T(8,128)S(1)} %fusion.27), kind=kOutput, calls=%fused_computation.10 | convolution fusion | flops 535729792 | bytes 4192768 | tf_op jit(solution)/shard_map/np,fpl->fnl/dot_general | solution.py:114
  76.5 1.9 %copy.63 = f32[3,1024,128]{2,1,0:T(8,128)S(1)} copy(f32[3,1024,128]{1,2,0:T(8,128)} %multiply_bitcast_fusion) | data formatting | bytes 3145728 | tf_op jit(solution)/shard_map/mul | solution.py:183
  78.4 1.0 %add_convert_fusion = bf16[3,64,16,128]{3,2,1,0:T(8,128)(2,1)} fusion(f32[3,64,16,128]{3,2,1,0:T(8,128)S(1)} %bitcast.110, bf16[3,64,16,128]{3,2,1,0:T(8,128)(2,1)S(1)} %copy-done), kind=kLoop, calls=%fused_computation.9 | loop fusion | flops 1179648 | bytes 3145728 | tf_op jit(solution)/shard_map/convert_element_type | solution.py:184
  (89 shorter events, 16.6 us)
Async XLA Ops:
  0.9 1.3 %copy-start.4 = (f32[4,64,16]{1,2,0:T(8,128)S(1)}, f32[4,64,16]{1,2,0:T(8,128)}, u32[]{:S(2)}) copy-start(f32[4,64,16]{1,2,0:T(8,128)} %param.9) | copy-start | bytes 49156
  4.1 1.0 %copy-start.5 = (f32[4,4,1,1]{1,0,3,2:T(4,128)S(1)}, f32[4,4,1,1]{1,0,3,2:T(4,128)}, u32[]{:S(2)}) copy-start(f32[4,4,1,1]{1,0,3,2:T(4,128)} %constant.12) | copy-start | bytes 196
  5.1 2.9 %copy-start.8 = (f32[64,16]{0,1:T(8,128)S(1)}, f32[64,16]{0,1:T(8,128)}, u32[]{:S(2)}) copy-start(f32[64,16]{0,1:T(8,128)} %param.10) | copy-start | bytes 12292
  19.8 3.8 %copy-start.1 = (f32[64,4,4]{2,1,0:T(4,128)S(1)}, f32[64,4,4]{2,1,0:T(4,128)}, u32[]{:S(2)}) copy-start(f32[64,4,4]{2,1,0:T(4,128)} %copy.49) | copy-start | bytes 12292
  19.8 3.9 %copy-start.2 = (f32[64,4,4]{2,1,0:T(4,128)S(1)}, f32[64,4,4]{2,1,0:T(4,128)}, u32[]{:S(2)}) copy-start(f32[64,4,4]{2,1,0:T(4,128)} %copy.48) | copy-start | bytes 12292
  19.8 3.9 %copy-start.3 = (f32[64,4,4]{2,1,0:T(4,128)S(1)}, f32[64,4,4]{2,1,0:T(4,128)}, u32[]{:S(2)}) copy-start(f32[64,4,4]{2,1,0:T(4,128)} %copy.54) | copy-start | bytes 12292
  26.2 2.1 %copy-start.6 = (f32[1024]{0:T(1024)S(1)}, f32[1024]{0:T(1024)}, u32[]{:S(2)}) copy-start(f32[1024]{0:T(1024)} %div.61) | copy-start | bytes 12292
  26.2 2.1 %copy-start.7 = (f32[1024]{0:T(1024)S(1)}, f32[1024]{0:T(1024)}, u32[]{:S(2)}) copy-start(f32[1024]{0:T(1024)} %div.58) | copy-start | bytes 12292
  29.3 1.0 %copy-start.9 = (s32[212]{0:T(256)S(1)}, s32[212]{0:T(256)}, u32[]{:S(2)}) copy-start(s32[212]{0:T(256)} %param.12) | copy-start | bytes 2548
  31.1 33.0 %copy-start.10 = (s32[212]{0:T(256)S(1)}, s32[212]{0:T(256)}, u32[]{:S(2)}) copy-start(s32[212]{0:T(256)} %param.13) | copy-start | bytes 2548
  31.1 33.6 %collective-permute-start.1 = (f32[3,99,128]{2,1,0:T(8,128)S(1)}, f32[3,99,128]{2,1,0:T(8,128)S(1)}, u32[]{:S(2)}, u32[]{:S(2)}) collective-permute-start(f32[3,99,128]{2,1,0:T(8,128)S(1)} %pad_maximum_fusion.1), channel_id=1, source_target_pairs={{0,24},{1,25},{2,26},{3,27},{4,28},{5,29},{6,30},{7,31},{8,0},{9,1... | collective-permute-start | bytes 456200 | tf_op jit(solution)/shard_map/ppermute | solution.py:20
  36.3 28.5 %collective-permute-start = (f32[3,99,128]{2,1,0:T(8,128)S(1)}, f32[3,99,128]{2,1,0:T(8,128)S(1)}, u32[]{:S(2)}, u32[]{:S(2)}) collective-permute-start(f32[3,99,128]{2,1,0:T(8,128)S(1)} %pad_maximum_fusion), channel_id=1, source_target_pairs={{0,8},{1,9},{2,10},{3,11},{4,12},{5,13},{6,14},{7,15},{8,16},{9,17... | collective-permute-start | bytes 456200 | tf_op jit(solution)/shard_map/ppermute | solution.py:20
  40.3 5.2 %collective-permute-start.5 = (f32[99]{0:T(128)S(1)}, f32[99]{0:T(128)S(1)}, u32[]{:S(2)}, u32[]{:S(2)}) collective-permute-start(f32[99]{0:T(128)S(1)} %pad_maximum_fusion.5), channel_id=1, source_target_pairs={{0,24},{1,25},{2,26},{3,27},{4,28},{5,29},{6,30},{7,31},{8,0},{9,1... | collective-permute-start | bytes 1196 | tf_op jit(solution)/shard_map/ppermute | solution.py:20
  45.4 5.4 %collective-permute-start.4 = (f32[99]{0:T(128)S(1)}, f32[99]{0:T(128)S(1)}, u32[]{:S(2)}, u32[]{:S(2)}) collective-permute-start(f32[99]{0:T(128)S(1)} %pad_maximum_fusion.4), channel_id=1, source_target_pairs={{0,8},{1,9},{2,10},{3,11},{4,12},{5,13},{6,14},{7,15},{8,16},{9,17... | collective-permute-start | bytes 1196 | tf_op jit(solution)/shard_map/ppermute | solution.py:20
  52.8 6.7 %collective-permute-start.6 = (f32[9]{0:T(128)S(1)}, f32[9]{0:T(128)S(1)}, u32[]{:S(2)}, u32[]{:S(2)}) collective-permute-start(f32[9]{0:T(128)S(1)} %pad_maximum_fusion.6), channel_id=1, source_target_pairs={{0,1},{1,2},{2,3},{3,4},{4,5},{5,6},{6,7},{7,8},{8,9},{9,10},{10,1... | collective-permute-start | bytes 116 | tf_op jit(solution)/shard_map/ppermute | solution.py:20
  55.7 5.1 %collective-permute-start.7 = (f32[9]{0:T(128)S(1)}, f32[9]{0:T(128)S(1)}, u32[]{:S(2)}, u32[]{:S(2)}) collective-permute-start(f32[9]{0:T(128)S(1)} %pad_maximum_fusion.7), channel_id=1, source_target_pairs={{0,31},{1,0},{2,1},{3,2},{4,3},{5,4},{6,5},{7,6},{8,7},{9,8},{10,9... | collective-permute-start | bytes 116 | tf_op jit(solution)/shard_map/ppermute | solution.py:20
  64.8 6.9 %collective-permute-start.2 = (f32[3,9,128]{2,1,0:T(8,128)S(1)}, f32[3,9,128]{2,1,0:T(8,128)S(1)}, u32[]{:S(2)}, u32[]{:S(2)}) collective-permute-start(f32[3,9,128]{2,1,0:T(8,128)S(1)} %pad_maximum_fusion.2), channel_id=1, source_target_pairs={{0,1},{1,2},{2,3},{3,4},{4,5},{5,6},{6,7},{7,8},{8,9},{9,10},{10,1... | collective-permute-start | bytes 41480 | tf_op jit(solution)/shard_map/ppermute | solution.py:20
  64.9 7.1 %collective-permute-start.3 = (f32[3,9,128]{2,1,0:T(8,128)S(1)}, f32[3,9,128]{2,1,0:T(8,128)S(1)}, u32[]{:S(2)}, u32[]{:S(2)}) collective-permute-start(f32[3,9,128]{2,1,0:T(8,128)S(1)} %pad_maximum_fusion.3), channel_id=1, source_target_pairs={{0,31},{1,0},{2,1},{3,2},{4,3},{5,4},{6,5},{7,6},{8,7},{9,8},{10,9... | collective-permute-start | bytes 41480 | tf_op jit(solution)/shard_map/ppermute | solution.py:20
  76.5 2.0 %copy-start = (bf16[3,64,16,128]{3,2,1,0:T(8,128)(2,1)S(1)}, bf16[3,64,16,128]{3,2,1,0:T(8,128)(2,1)}, u32[]{:S(2)}) copy-start(bf16[3,64,16,128]{3,2,1,0:T(8,128)(2,1)} %param.8) | copy-start | bytes 2359300
where the time goes:
time: 80 us; the launch traced here: 79.5 us
  local copies, waits for them, and re-layouts  22 us (28%)
  matrix products  21.2 us (26%)
  starting transfers between devices  20 us (25%)
  other arithmetic  9.03 us (11%)
  waiting for transfers between devices  6.75 us (8%)
    ppermute x8, starting transfers between devices, from_behind(): return lax.ppermute(value, axis, pairs)  20 us
    dot_general x3, matrix products, along_cols(): jnp.einsum('aj,erjl->eral', derivative, values, precision=lax.Precision.H...  8.39 us
    ppermute x8, waiting for transfers between devices, from_behind(): return lax.ppermute(value, axis, pairs)  6.75 us
    concatenate x4, other arithmetic, local(): masses_cat = jnp.concatenate([section[1] for section in sections], axis=0)  5.44 us
    dot_general x7, matrix products, split_dot(): first = jnp.einsum(form, table, upper, preferred_element_type=jnp.float32)  5.07 us
    div x4, local copies, waits for them, and re-layouts, element_tendency(): (weights[:, None] * weights[None, :])[None] / jacobian_inv[..., 0]  4.35 us
    dot_general x7, matrix products, split_dot(): jnp.einsum(form, table, lower, preferred_element_type=jnp.float32)  3.89 us
    dot_general x3, matrix products, along_rows(): jnp.einsum('aj,ejcl->eacl', derivative, values, precision=lax.Precision.H...  3.87 us
  transfers between devices with their start and end apart: 8, of which 4 were waited for; matrix products, arithmetic and copies ran while one was open for 18% of the time, Pallas kernels for 0%

commit v1 on v0

v1 whole, which is shorter than its diff:
```python
import functools
import math

import jax
import jax.numpy as jnp
import numpy as np
from jax import lax
from jax.experimental import pallas as pl
from jax.experimental.pallas import tpu as pltpu
from jax.sharding import PartitionSpec as P

BX = 32
BY = 2
STEP_SIZE = 0.1
ROWS = 256
LANES = 128
F32 = jnp.float32
BF16 = jnp.bfloat16
MESH = pl.DeviceIdType.MESH


def gll_tables():
    abscissa = np.array([-1.0, -math.sqrt(0.2), math.sqrt(0.2), 1.0])
    legendre = 0.5 * (5.0 * abscissa * abscissa * abscissa - 3.0 * abscissa)
    derivative = np.zeros((4, 4))
    for target in range(4):
        for source in range(4):
            if target != source:
                derivative[target, source] = legendre[target] / (
                    legendre[source] * (abscissa[target] - abscissa[source])
                )
    derivative[0, 0] = -3.0
    derivative[3, 3] = 3.0
    weights = np.array([1.0, 5.0, 5.0, 1.0]) / 6.0
    return (derivative, weights)


def round_bf16(values):
    return np.asarray(values, dtype=jnp.bfloat16).astype(np.float64)


def operator_tables():
    derivative, weights = gll_tables()
    eye4 = np.eye(4)
    node_weight = np.kron(weights, weights)
    along_c = node_weight[:, None] * np.kron(eye4, derivative)
    along_r = node_weight[:, None] * np.kron(derivative, eye4)
    best = None
    for trial in np.linspace(1.0, 2.0, 2001)[:-1]:
        error = max(
            np.max(np.abs(round_bf16(trial * t) / trial - t) / (np.abs(t).max(1, keepdims=True)))
            for t in (along_c, along_r)
        )
        if best is None or error < best[0]:
            best = (error, trial)
    scale = float(best[1])
    eye = np.eye(ROWS // 16)
    stacked = np.concatenate([np.kron(eye, along_c), np.kron(eye, along_r)], axis=0) * scale
    return np.asarray(stacked, dtype=np.float32), scale


def link_groups(lap_blocks):
    side_points = 3 * BY + 1
    top_points = 3 * BX + 1
    group_sizes = [
        (1, side_points),
        (-1, side_points),
        (lap_blocks, top_points),
        (-lap_blocks, top_points),
        (lap_blocks + 1, 1),
        (-lap_blocks - 1, 1),
        (lap_blocks - 1, 1),
        (1 - lap_blocks, 1),
    ]
    groups = []
    first_slot = 0
    first_row = 0
    for offset, slot_count in group_sizes:
        padded = -(-slot_count // 8) * 8
        groups.append((offset, first_slot, slot_count, first_row, padded))
        first_slot += slot_count
        first_row += padded
    return groups, first_row


def iota(shape, dim):
    return lax.broadcasted_iota(jnp.int32, shape, dim)


def dot(a, b):
    return lax.dot_general(a, b, (((1,), (0,)), ((), ())), preferred_element_type=F32)


def dot_nt(a, b):
    return lax.dot_general(a, b, (((1,), (1,)), ((), ())), preferred_element_type=F32)


def kernel(
    sizes, groups, slots, scale,
    prog_hbm, metric_hbm, cor_hbm, node_hbm, send_hbm, recv_hbm, ops_hbm,
    out_hbm,
    prog, metric, cor, node, sendp, recvp, ops,
    wide, weighted, summed, inverse, table_s, table_r,
    outgoing, arrived, out_mass, arrived_mass, result,
    in_sem, out_sem, send_sem, recv_sem, msend_sem, mrecv_sem,
):
    nface, nsub = sizes
    total = nface * nsub
    nodes = prog.shape[1]
    blocks = nodes // ROWS
    me = lax.axis_index("face") * nsub + lax.axis_index("sub")
    peers = []
    for offset, *_ in groups:
        other = lax.rem(me + (offset % total), total)
        peers.append((other // nsub, lax.rem(other, nsub)))

    barrier = pltpu.get_barrier_semaphore()
    for peer in peers:
        pl.semaphore_signal(barrier, inc=1, device_id=peer, device_id_type=MESH)

    loads = []
    for k, (src, dst) in enumerate((
        (metric_hbm, metric), (cor_hbm, cor), (node_hbm, node),
        (send_hbm, sendp), (recv_hbm, recvp), (prog_hbm, prog), (ops_hbm, ops),
    )):
        copy = pltpu.make_async_copy(src, dst, in_sem.at[k])
        copy.start()
        loads.append(copy)
    for copy in loads[:5]:
        copy.wait()

    elements = node.shape[1]
    a, b, e, g = metric[0], metric[1], metric[2], metric[3]
    inv_det = 1.0 / (a * g - b * e)
    lane16 = iota((16, 1), 0)
    col, row = lane16 & 3, lane16 >> 2
    w_node = jnp.where((col == 0) | (col == 3), 1 / 6, 5 / 6) * jnp.where((row == 0) | (row == 3), 1 / 6, 5 / 6)
    mass = w_node * inv_det
    compact = jnp.concatenate(
        [a * inv_det, b * inv_det, e * inv_det, g * inv_det, scale * (mass * cor[...]), mass,
         node[...].astype(F32), jnp.zeros((16, elements), F32)], axis=0).T
    upper = compact.astype(BF16).astype(F32)
    both = jnp.concatenate([upper, compact - upper], axis=1)
    own = (iota((16, 2 * LANES), 1) & 15) == iota((16, 2 * LANES), 0)
    spread = jnp.where(own[None], jnp.broadcast_to(both[:, None, :], (elements, 16, 2 * LANES)), 0.0)
    spread = spread.reshape(nodes, 2 * LANES).astype(BF16)
    pick_l = (iota((2 * LANES, 7 * LANES), 0) & (LANES - 1)) >> 4
    pick = (pick_l == (iota((2 * LANES, 7 * LANES), 1) >> 7)).astype(F32).astype(BF16)
    row_l = (iota((8, 2 * LANES), 1) & (LANES - 1)) >> 4
    point_row = dot_nt((row_l == 6).astype(F32).astype(BF16), spread)[0:1]
    mass_row = dot_nt((row_l == 5).astype(F32).astype(BF16), spread).astype(BF16)
    wide[...] = dot(spread, pick)
    weighted[:, 3 * LANES:] = wide[:, 5 * LANES:6 * LANES].astype(BF16)

    count = sendp.shape[1]
    padded = iota((slots, 1), 0)
    slot_of = jnp.full((slots, 1), -1, jnp.int32)
    for _, first_slot, slot_count, first_row, _ in groups:
        inside = (padded >= first_row) & (padded < first_row + slot_count)
        slot_of = jnp.where(inside, padded - first_row + first_slot, slot_of)
    chosen = slot_of == iota((slots, count), 1)
    vacant = jnp.where(slot_of < 0, -1.0, 0.0)
    send_col = jnp.sum(jnp.where(chosen, sendp[...].astype(F32), 0.0), axis=1, keepdims=True) + vacant
    recv_col = jnp.sum(jnp.where(chosen, recvp[...].astype(F32), 0.0), axis=1, keepdims=True) + vacant
    same = iota((slots, slots), 0) == iota((slots, slots), 1)
    recv_row = jnp.sum(jnp.where(same, recv_col, 0.0), axis=0, keepdims=True)
    table_s[...] = jnp.where(send_col == point_row, 1.0, 0.0).astype(BF16)
    out_mass[...] = dot_nt(mass_row, table_s[...])

    pl.semaphore_wait(barrier, len(peers))
    sends = []
    mass_copies = []
    for k in range(len(groups)):
        copy = pltpu.make_async_remote_copy(
            src_ref=out_mass, dst_ref=arrived_mass.at[k],
            send_sem=msend_sem.at[k], recv_sem=mrecv_sem.at[k],
            device_id=peers[k], device_id_type=MESH)
        copy.start()
        mass_copies.append(copy)
    order = [k for k in range(len(groups)) if k not in (2, 3)] + [2, 3]

    def field_copy(field, k):
        first_row, size = groups[k][3], groups[k][4]
        return pltpu.make_async_remote_copy(
            src_ref=outgoing.at[field, pl.ds(first_row, size)],
            dst_ref=arrived.at[field, pl.ds(first_row, size)],
            send_sem=send_sem.at[field, k], recv_sem=recv_sem.at[field, k],
            device_id=peers[k], device_id_type=MESH)

    copies = {}

    def send_field(field):
        for k in order:
            copies[field, k] = field_copy(field, k)
            copies[field, k].start()

    loads[5].wait()
    loads[6].wait()
    along_c = ops[:ROWS]
    along_r = ops[ROWS:]

    def read(block):
        rows = pl.ds(block * ROWS, ROWS)
        fields = [prog[f, rows].astype(F32) for f in range(3)]
        coefs = [wide[rows, k * LANES:(k + 1) * LANES] for k in range(5)]
        return rows, fields, coefs

    for pair in range(0, blocks, 2):
        one, two = [], []
        for block in (pair, pair + 1):
            _, (u1, u2, phi), (ca, cb, ce, cg, _) = read(block)
            one.append((phi * (ca * u1 + cb * u2)).astype(BF16))
            two.append((phi * (ce * u1 + cg * u2)).astype(BF16))
        div = dot(along_c, jnp.concatenate(one, axis=1)) + dot(along_r, jnp.concatenate(two, axis=1))
        for j, block in enumerate((pair, pair + 1)):
            weighted[pl.ds(block * ROWS, ROWS), 2 * LANES:3 * LANES] = (
                -div[:, j * LANES:(j + 1) * LANES]).astype(BF16)
    outgoing[2] = dot(table_s[...], weighted[:, 2 * LANES:3 * LANES])
    send_field(2)

    for pair in range(0, blocks, 2):
        one, two, energy = [], [], []
        for block in (pair, pair + 1):
            _, (u1, u2, phi), (ca, cb, ce, cg, _) = read(block)
            one.append((ca * u2 - cb * u1).astype(BF16))
            two.append((ce * u2 - cg * u1).astype(BF16))
            energy.append((0.5 * (u1 * u1 + u2 * u2) + phi).astype(BF16))
        energy = jnp.concatenate(energy, axis=1)
        vort = dot(along_c, jnp.concatenate(one, axis=1)) + dot(along_r, jnp.concatenate(two, axis=1))
        ref1 = dot(along_c, energy)
        ref2 = dot(along_r, energy)
        for j, block in enumerate((pair, pair + 1)):
            rows, (u1, u2, _), (ca, cb, ce, cg, cf) = read(block)
            lanes = slice(j * LANES, (j + 1) * LANES)
            eta = vort[:, lanes] + cf
            x1, x2 = ref1[:, lanes], ref2[:, lanes]
            weighted[rows, 0:LANES] = (eta * u2 - (ca * x1 + ce * x2)).astype(BF16)
            weighted[rows, LANES:2 * LANES] = (-(eta * u1) - (cb * x1 + cg * x2)).astype(BF16)
    pair_out = dot(table_s[...], weighted[:, 0:2 * LANES])
    outgoing[0] = pair_out[:, :LANES]
    outgoing[1] = pair_out[:, LANES:]
    send_field(0)
    send_field(1)

    for block in range(blocks):
        rows = pl.ds(block * ROWS, ROWS)
        point = wide[rows, 6 * LANES:7 * LANES][:, 0:1]
        meet = jnp.where(point == point_row, 1.0, 0.0).astype(BF16)
        summed[rows, :] = dot(meet, weighted[...])

    for copy in mass_copies:
        copy.wait_recv()
    lane = iota((1, slots), 1)
    mass_in = jnp.zeros((1, slots), F32)
    for k, (_, _, _, first_row, size) in enumerate(groups):
        inside = (lane >= first_row) & (lane < first_row + size)
        mass_in = jnp.where(inside, arrived_mass[k, 0:1, :], mass_in)
    ones = jnp.ones((slots, LANES), BF16)
    for block in range(blocks):
        rows = pl.ds(block * ROWS, ROWS)
        point = wide[rows, 6 * LANES:7 * LANES][:, 0:1]
        hit = point == recv_row
        table_r[rows, :] = jnp.where(hit, 1.0, 0.0).astype(BF16)
        far = dot(jnp.where(hit, mass_in, 0.0).astype(BF16), ones)
        inv = (STEP_SIZE / scale) / (summed[rows, 3 * LANES:] + far)
        inverse[rows, :] = inv
        for f in range(3):
            lanes = slice(f * LANES, (f + 1) * LANES)
            summed[rows, lanes] = prog[f, rows].astype(F32) + inv * summed[rows, lanes]

    stores = []
    for f in (2, 0, 1):
        for k in order:
            copies[f, k].wait_recv()
        landed = arrived[f].astype(BF16)
        for block in range(blocks):
            rows = pl.ds(block * ROWS, ROWS)
            far = dot(table_r[rows, :], landed)
            value = summed[rows, f * LANES:(f + 1) * LANES] + inverse[rows, :] * far
            result[f, rows] = value.astype(BF16)
        copy = pltpu.make_async_copy(result.at[f], out_hbm.at[f], out_sem.at[f])
        copy.start()
        stores.append(copy)
    for copy in mass_copies:
        copy.wait_send()
    for copy in copies.values():
        copy.wait_send()
    for copy in stores:
        copy.wait()


def local(prognostic, metric, coriolis, node_point, send_point, recv_point):
    elements, per, levels = prognostic.shape[1:]
    nodes = elements * per
    sizes = (lax.axis_size("face"), lax.axis_size("sub"))
    groups, slots = link_groups(4 * sizes[1])
    tables, scale = operator_tables()
    links = send_point.shape[0]
    any_spec = pl.BlockSpec(memory_space=pl.ANY)
    dma = pltpu.SemaphoreType.DMA
    vmem = pltpu.VMEM
    out = pl.pallas_call(
        functools.partial(kernel, sizes, groups, slots, scale),
        out_shape=jax.ShapeDtypeStruct((3, nodes, levels), BF16),
        in_specs=[any_spec] * 7,
        out_specs=any_spec,
        scratch_shapes=[
            vmem((3, nodes, levels), BF16),
            vmem((4, per, elements), F32),
            vmem((per, elements), F32),
            vmem((per, elements), jnp.int32),
            vmem((1, links), jnp.int32),
            vmem((1, links), jnp.int32),
            vmem((2 * ROWS, ROWS), BF16),
            vmem((nodes, 7 * LANES), F32),
            vmem((nodes, 4 * LANES), BF16),
            vmem((nodes, 4 * LANES), F32),
            vmem((nodes, LANES), F32),
            vmem((slots, nodes), BF16),
            vmem((nodes, slots), BF16),
            vmem((3, slots, levels), F32),
            vmem((3, slots, levels), F32),
            vmem((8, slots), F32),
            vmem((len(groups), 8, slots), F32),
            vmem((3, nodes, levels), BF16),
            dma((7,)),
            dma((3,)),
            dma((3, len(groups))),
            dma((3, len(groups))),
            dma((len(groups),)),
            dma((len(groups),)),
        ],
        compiler_params=pltpu.CompilerParams(collective_id=0, has_side_effects=True),
    )(
        prognostic.reshape(3, nodes, levels), metric.swapaxes(1, 2), coriolis.T, node_point.T,
        send_point.reshape(1, links), recv_point.reshape(1, links),
        jnp.asarray(tables, dtype=BF16),
    )
    return out.reshape(3, elements, per, levels)


def solution(mesh):
    placed = (
        P(None, ("face", "sub"), None, None),
        P(None, ("face", "sub"), None),
        P(("face", "sub"), None),
        P(("face", "sub"), None),
        P(("face", "sub")),
        P(("face", "sub")),
    )
    return jax.shard_map(
        local,
        mesh=mesh,
        in_specs=placed,
        out_specs=P(None, ("face", "sub"), None, None),
        check_vma=False,
    )
```

time: 80 us -> 20.4 us (0.26)
  matrix products: 21.2 us -> 0 us
  starting transfers between devices: 20 us -> 0 us
  local copies, waits for them, and re-layouts: 22 us -> 2.15 us
  Pallas kernels: 0 us -> 18 us
  other arithmetic: 9.03 us -> 0 us
  waiting for transfers between devices: 6.75 us -> 0 us
    dot_general x20 -> x0, matrix products: 21.2 us -> none  [the longest x3 8.39 us: along_cols(): jnp.einsum('aj,erjl->eral', derivative, values, precision=lax.Precision.H...]
    ppermute x8 -> x0, starting transfers between devices: 20 us -> none  [from_behind(): return lax.ppermute(value, axis, pairs)]
    pallas_call x0 -> x1, Pallas kernels: none -> 18 us  [local(): pl.pallas_call(functools.partial(kernel, sizes, groups, slots, scale), ou...]
    ppermute x8 -> x0, waiting for transfers between devices: 6.75 us -> none  [from_behind(): return lax.ppermute(value, axis, pairs)]
    concatenate x8 -> x0, other arithmetic: 5.5 us -> none  [the longest x4 5.44 us: local(): masses_cat = jnp.concatenate([section[1] for section in sections], axis=0)]
    slice x17 -> x0, local copies, waits for them, and re-layouts: 4.75 us -> none  [the longest x4 2.57 us: split_bundle(): bundle[1][cursor:cursor + slot_count]]
    mul x5 -> x0, local copies, waits for them, and re-layouts: 4.56 us -> none  [the longest x4 2.62 us: element_tendency(): weights[:, None] * weights[None, :]]
    div x4 -> x0, local copies, waits for them, and re-layouts: 4.35 us -> none  [element_tendency(): (weights[:, None] * weights[None, :])[None] / jacobian_inv[..., 0]]
  transfers between devices with their start and end apart: 8 -> 0, of which waited for: 4 -> 0; matrix products, arithmetic and copies ran while one was open for 18% -> 0% of each run, Pallas kernels for 0% -> 0%
where the time goes in v1:
time: 20.4 us; the launch traced here: 20.2 us
  Pallas kernels  18 us (88%)
  local copies, waits for them, and re-layouts  2.15 us (11%)
    pallas_call x1, Pallas kernels, local(): pl.pallas_call(functools.partial(kernel, sizes, groups, slots, scale), ou...  18 us
    unnamed x1, local copies, waits for them, and re-layouts  2.15 us

profile of v1, /device:TPU:0, one launch (start us, length us, event | category | flops | bytes accessed | tf_op | source)
XLA Modules:
  0.0 20.2 jit_solution(17813920847081875719)
XLA Ops:
  0.0 18.0 %shard_map.73 = bf16[3,1024,128]{2,1,0:T(8,128)(2,1)} custom-call(bf16[3,1024,128]{2,1,0:T(8,128)(2,1)} %bitcast.8, f32[4,16,64]{2,1,0:T(8,128)} %bitcast.9, f32[16,64]{1,0:T(8,128)} %bitcast.10, s32[16,64]{1,0:T(8,128)} %bitcast.11, s32[1,212]{1,0:T(1,128)} %bitcast.12, s32[1,212]{1,0:T(1,128)} %bitcast.13, bf16[512,256]{1,0:T(8,128)(2,1)} %constant.2.clone.ops_hbm), custom_call_target="tpu_custom_call" | custom-call | tf_op jit(solution)/shard_map/pallas_call | solution.py:302
  18.1 2.1 %copy.9 = bf16[3,64,16,128]{3,2,1,0:T(8,128)(2,1)} copy(bf16[3,64,16,128]{3,2,1,0:T(8,128)(2,1)} %bitcast.7) | data formatting | bytes 1572864

commit v2 on v1

--- a/solution.py
+++ b/solution.py
@@ -95,14 +95,18 @@
     return lax.dot_general(a, b, (((1,), (1,)), ((), ())), preferred_element_type=F32)
 
 
+def wait_bytes(ref, sem):
+    pltpu.make_async_copy(ref, ref, sem).wait()
+
+
 def kernel(
     sizes, groups, slots, scale,
     prog_hbm, metric_hbm, cor_hbm, node_hbm, send_hbm, recv_hbm, ops_hbm,
     out_hbm,
     prog, metric, cor, node, sendp, recvp, ops,
     wide, weighted, summed, inverse, table_s, table_r,
-    outgoing, arrived, out_mass, arrived_mass, result,
-    in_sem, out_sem, send_sem, recv_sem, msend_sem, mrecv_sem,
+    outgoing, arrived, out_mass, arrived_mass,
+    in_sem, send_sem, recv_sem, msend_sem, mrecv_sem,
 ):
     nface, nsub = sizes
     total = nface * nsub
@@ -114,6 +118,7 @@
         other = lax.rem(me + (offset % total), total)
         peers.append((other // nsub, lax.rem(other, nsub)))
 
+    arrived[...] = jnp.zeros_like(arrived)
     barrier = pltpu.get_barrier_semaphore()
     for peer in peers:
         pl.semaphore_signal(barrier, inc=1, device_id=peer, device_id_type=MESH)
@@ -165,34 +170,28 @@
     same = iota((slots, slots), 0) == iota((slots, slots), 1)
     recv_row = jnp.sum(jnp.where(same, recv_col, 0.0), axis=0, keepdims=True)
     table_s[...] = jnp.where(send_col == point_row, 1.0, 0.0).astype(BF16)
-    out_mass[...] = dot_nt(mass_row, table_s[...])
+    out_mass[...] = dot_nt(mass_row, table_s[...])[0:1]
 
     pl.semaphore_wait(barrier, len(peers))
-    sends = []
-    mass_copies = []
     for k in range(len(groups)):
         copy = pltpu.make_async_remote_copy(
             src_ref=out_mass, dst_ref=arrived_mass.at[k],
-            send_sem=msend_sem.at[k], recv_sem=mrecv_sem.at[k],
+            send_sem=msend_sem.at[0], recv_sem=mrecv_sem.at[0],
             device_id=peers[k], device_id_type=MESH)
         copy.start()
-        mass_copies.append(copy)
     order = [k for k in range(len(groups)) if k not in (2, 3)] + [2, 3]
 
     def field_copy(field, k):
-        first_row, size = groups[k][3], groups[k][4]
+        used, first_row = groups[k][2], groups[k][3]
         return pltpu.make_async_remote_copy(
-            src_ref=outgoing.at[field, pl.ds(first_row, size)],
-            dst_ref=arrived.at[field, pl.ds(first_row, size)],
-            send_sem=send_sem.at[field, k], recv_sem=recv_sem.at[field, k],
+            src_ref=outgoing.at[field, pl.ds(first_row, used)],
+            dst_ref=arrived.at[field, pl.ds(first_row, used)],
+            send_sem=send_sem.at[field], recv_sem=recv_sem.at[field],
             device_id=peers[k], device_id_type=MESH)
-
-    copies = {}
 
     def send_field(field):
         for k in order:
-            copies[field, k] = field_copy(field, k)
-            copies[field, k].start()
+            field_copy(field, k).start()
 
     loads[5].wait()
     loads[6].wait()
@@ -248,8 +247,7 @@
         meet = jnp.where(point == point_row, 1.0, 0.0).astype(BF16)
         summed[rows, :] = dot(meet, weighted[...])
 
-    for copy in mass_copies:
-        copy.wait_recv()
+    wait_bytes(arrived_mass, mrecv_sem.at[0])
     lane = iota((1, slots), 1)
     mass_in = jnp.zeros((1, slots), F32)
     for k, (_, _, _, first_row, size) in enumerate(groups):
@@ -268,25 +266,17 @@
             lanes = slice(f * LANES, (f + 1) * LANES)
             summed[rows, lanes] = prog[f, rows].astype(F32) + inv * summed[rows, lanes]
 
-    stores = []
     for f in (2, 0, 1):
-        for k in order:
-            copies[f, k].wait_recv()
+        wait_bytes(arrived.at[f, pl.ds(0, count)], recv_sem.at[f])
         landed = arrived[f].astype(BF16)
         for block in range(blocks):
             rows = pl.ds(block * ROWS, ROWS)
             far = dot(table_r[rows, :], landed)
             value = summed[rows, f * LANES:(f + 1) * LANES] + inverse[rows, :] * far
-            result[f, rows] = value.astype(BF16)
-        copy = pltpu.make_async_copy(result.at[f], out_hbm.at[f], out_sem.at[f])
-        copy.start()
-        stores.append(copy)
-    for copy in mass_copies:
-        copy.wait_send()
-    for copy in copies.values():
-        copy.wait_send()
-    for copy in stores:
-        copy.wait()
+            out_hbm[f, rows] = value
+    wait_bytes(arrived_mass, msend_sem.at[0])
+    for f in range(3):
+        wait_bytes(outgoing.at[f, pl.ds(0, count)], send_sem.at[f])
 
 
 def local(prognostic, metric, coriolis, node_point, send_point, recv_point):
@@ -296,14 +286,14 @@
     groups, slots = link_groups(4 * sizes[1])
     tables, scale = operator_tables()
     links = send_point.shape[0]
-    any_spec = pl.BlockSpec(memory_space=pl.ANY)
+    any_spec = pl.BlockSpec(memory_space=pltpu.HBM)
     dma = pltpu.SemaphoreType.DMA
     vmem = pltpu.VMEM
     out = pl.pallas_call(
         functools.partial(kernel, sizes, groups, slots, scale),
-        out_shape=jax.ShapeDtypeStruct((3, nodes, levels), BF16),
+        out_shape=pltpu.VMEM((3, nodes, levels), F32),
         in_specs=[any_spec] * 7,
-        out_specs=any_spec,
+        out_specs=pl.BlockSpec(memory_space=pltpu.VMEM),
         scratch_shapes=[
             vmem((3, nodes, levels), BF16),
             vmem((4, per, elements), F32),
@@ -320,23 +310,22 @@
             vmem((nodes, slots), BF16),
             vmem((3, slots, levels), F32),
             vmem((3, slots, levels), F32),
-            vmem((8, slots), F32),
-            vmem((len(groups), 8, slots), F32),
-            vmem((3, nodes, levels), BF16),
+            vmem((1, slots), F32),
+            vmem((len(groups), 1, slots), F32),
             dma((7,)),
             dma((3,)),
-            dma((3, len(groups))),
-            dma((3, len(groups))),
-            dma((len(groups),)),
-            dma((len(groups),)),
+            dma((3,)),
+            dma((1,)),
+            dma((1,)),
         ],
-        compiler_params=pltpu.CompilerParams(collective_id=0, has_side_effects=True),
+        compiler_params=pltpu.CompilerParams(
+            collective_id=0, has_side_effects=True),
     )(
         prognostic.reshape(3, nodes, levels), metric.swapaxes(1, 2), coriolis.T, node_point.T,
         send_point.reshape(1, links), recv_point.reshape(1, links),
         jnp.asarray(tables, dtype=BF16),
     )
-    return out.reshape(3, elements, per, levels)
+    return out.astype(BF16).reshape(3, elements, per, levels)
 
 
 def solution(mesh):

time: 20.4 us -> 16.5 us (0.81)
  Pallas kernels: 18 us -> 15.4 us
  local copies, waits for them, and re-layouts: 2.15 us -> 0 us
  other arithmetic: 0 us -> 0.98 us
    pallas_call x1, Pallas kernels: 18 us -> 15.4 us  [local(): pl.pallas_call(functools.partial(kernel, sizes, groups, slots, scale), ou...]
    unnamed x1 -> x0, local copies, waits for them, and re-layouts: 2.15 us -> none
    convert_element_type x0 -> x1, other arithmetic: none -> 0.98 us  [local(): return out.astype(BF16).reshape(3, elements, per, levels)]
where the time goes in v2:
time: 16.5 us; the launch traced here: 16.4 us
  Pallas kernels  15.4 us (93%)
  other arithmetic  0.98 us (6%)
    pallas_call x1, Pallas kernels, local(): pl.pallas_call(functools.partial(kernel, sizes, groups, slots, scale), ou...  15.4 us
    convert_element_type x1, other arithmetic, local(): return out.astype(BF16).reshape(3, elements, per, levels)  0.98 us

profile of v2, /device:TPU:0, one launch (start us, length us, event | category | flops | bytes accessed | tf_op | source)
XLA Modules:
  0.0 16.4 jit_solution(12627563905529443250)
XLA Ops:
  0.0 15.4 %shard_map.73 = f32[3,1024,128]{2,1,0:T(8,128)S(1)} custom-call(bf16[3,1024,128]{2,1,0:T(8,128)(2,1)} %bitcast.7, f32[4,16,64]{2,1,0:T(8,128)} %bitcast.8, f32[16,64]{1,0:T(8,128)} %bitcast.9, s32[16,64]{1,0:T(8,128)} %bitcast.10, s32[1,212]{1,0:T(1,128)} %bitcast.11, s32[1,212]{1,0:T(1,128)} %bitcast.12, bf16[512,256]{1,0:T(8,128)(2,1)} %constant.2.clone.ops_hbm), custom_call_target="tpu_custom_call" | custom-call | tf_op jit(solution)/shard_map/pallas_call | solution.py:292
  15.4 1.0 %convert_element_type.3 = bf16[3,1024,128]{2,1,0:T(8,128)(2,1)} convert(f32[3,1024,128]{2,1,0:T(8,128)S(1)} %shard_map.73) | non-fusion elementwise | flops 393216 | bytes 2359296 | tf_op jit(solution)/shard_map/convert_element_type | solution.py:328
